TPU v7x, 32 devices: a whole 2x2x4 slice. The times are simulated.
32 devices in a mesh: row: 8 (over z, y), col: 4 (over x, core).
Axes of the slice: x: 2, y: 2, z: 4, core: 2. Of those that a mesh axis runs over, the one named last changes fastest.
Arguments:
- densities: bfloat16 [4608, 3072], P(('row', 'col')), may hold values from -0.796875 to 0.796875
- counts: int32 [512], P(('row', 'col')), may hold values from 3 to 9
- coulomb: float32 [3072], replicated, may hold values from 0.05 to 1
- energies: float32 [4608], P(('row', 'col')), may hold values from 8 to 64
- vectors: bfloat16 [4608, 64], P(('row', 'col')), may hold values from -0.09375 to 0.09375
Outputs:
- kernel: float32 [4608, 4608], P('row', 'col')
- product: float32 [4608, 64], P(('row', 'col'))
All inputs are finite; a program needn't handle non-finite values.
Results may differ from a plain program's by a relative error of at most 0.0095.
Values may be sent and summed in bfloat16 or wider, within the bound.
A program may use at most 128 MiB of HBM per device.

v0:
```python
import jax
import jax.numpy as jnp
from jax import lax
from jax.sharding import PartitionSpec as P

SLOT = 9


def body(densities, counts, coulomb, energies, vectors):
    kpoints = counts.shape[0]
    slot_index = lax.broadcasted_iota(jnp.int32, (kpoints, SLOT), 1)
    usable = (slot_index < counts[:, None]).reshape(kpoints * SLOT)
    masked = jnp.where(usable[:, None], densities, jnp.zeros_like(densities))
    weighted = (masked.astype(jnp.float32) * coulomb[None, :]).astype(jnp.bfloat16)
    row_block = lax.all_gather(weighted, "col", axis=0, tiled=True)
    kernel = lax.dot_general(
        row_block,
        lax.all_gather(masked, "row", axis=0, tiled=True),
        (((1,), (1,)), ((), ())),
        preferred_element_type=jnp.float32,
    )
    local_terms = lax.dot_general(
        masked, vectors, (((0,), (0,)), ((), ())), preferred_element_type=jnp.float32
    )
    projected = lax.psum(local_terms, ("row", "col"))
    coupled = jnp.dot(
        weighted.astype(jnp.float32),
        projected,
        precision=lax.Precision.HIGHEST,
        preferred_element_type=jnp.float32,
    )
    diagonal = jnp.where(usable, energies, jnp.zeros_like(energies))
    product = coupled + diagonal[:, None] * vectors.astype(jnp.float32)
    return (kernel, product)


def solution(mesh):
    return jax.shard_map(
        body,
        mesh=mesh,
        in_specs=(
            P(("row", "col"), None),
            P(("row", "col")),
            P(),
            P(("row", "col")),
            P(("row", "col"), None),
        ),
        out_specs=(P("row", "col"), P(("row", "col"), None)),
        check_vma=False,
    )
```

profile of v0, /device:TPU:0, one launch (start us, length us, event | category | flops | bytes accessed | tf_op | source)
XLA Modules:
  0.0 254.9 jit_solution(2723518301834246498)
XLA Ops:
  8.0 0.0 copy-start.2
  8.0 0.0 all-reduce.2.cloned.1.call-start
  8.1 0.7 iota_compare_fusion
  8.8 0.1 lt.18
  8.9 2.5 multiply_convert_fusion
  11.4 0.0 copy-start
  11.4 0.0 copy-done.2
  11.4 0.0 copy-start.3
  11.4 0.0 copy-start.1
  11.4 1.8 fusion.1
  13.2 0.0 all-reduce.2.cloned.1.call-update
  13.2 0.0 all-gather.3.cloned.1.call-start
  13.3 0.5 all-gather.3.cloned.1.call-update
  13.8 0.0 all-gather.5.cloned.1.call-start
  13.9 0.0 copy-done
  13.9 0.5 all-gather.5.cloned.1.call-update
  14.4 0.0 copy-done.3
  14.4 219.2 %all-reduce.2.cloned.1.call-done = f32[3072,64]{1,0:T(8,128)} async-done(((f32[3072,64]{1,0:T(8,128)}), f32[3072,64]{1,0:T(8,128)}) %all-reduce.2.cloned.1.call-update) | async-done | bytes 786448 | tf_op jit(solution)/shard_map/psum | solution.py:25
  233.7 0.0 copy-done.1
  233.7 3.5 %convolution_add_fusion = f32[144,64]{0,1:T(8,128)} fusion(bf16[144,3072]{1,0:T(8,128)(2,1)S(1)} %copy-done.1, f32[3072,64]{1,0:T(8,128)} %all-reduce.2.cloned.1.call-done, bf16[144,64]{0,1:T(8,128)(2,1)S(1)} %copy-done.2, f32[144]{0:T(256)S(1)} %broadcast_select_fusion.1), kind=kOutput, calls=%fused_computation.1 | convolution fusion | flops 339766272 | bytes 1727040 | tf_op jit(solution)/shard_map/dot_general | solution.py:26
  237.1 0.0 all-gather.3.cloned.1.call-done
  237.1 0.0 all-gather.5.cloned.1.call-done
  237.1 10.4 %fusion = f32[576,1152]{1,0:T(8,128)} fusion(bf16[576,3072]{1,0:T(8,128)(2,1)} %all-gather.3.cloned.1.call-done, bf16[1152,3072]{1,0:T(8,128)(2,1)} %all-gather.5.cloned.1.call-done), kind=kOutput, calls=%fused_computation.5 | convolution fusion | flops 4076863488 | bytes 13271040 | tf_op jit(solution)/shard_map/dot_general | solution.py:16
  (1 shorter events, 0.0 us)
Async XLA Ops:
  8.0 3.4 %copy-start.2 = (bf16[144,64]{0,1:T(8,128)(2,1)S(1)}, bf16[144,64]{0,1:T(8,128)(2,1)}, u32[]{:S(2)}) copy-start(bf16[144,64]{0,1:T(8,128)(2,1)} %param.9) | copy-start | bytes 55300
  8.0 225.6 %all-reduce.2.cloned.1.call-start = ((), (), s32[]{:S(2)}) async-start(), calls=%async_computation.2 | async-start | bytes 3145728 | tf_op jit(solution)/shard_map/psum | solution.py:25
  11.4 2.5 copy-start
  11.4 3.0 %copy-start.3 = (f32[144]{0:T(256)S(1)}, f32[144]{0:T(256)}, u32[]{:S(2)}) copy-start(f32[144]{0:T(256)} %param.8) | copy-start | bytes 1732
  11.4 222.2 %copy-start.1 = (bf16[144,3072]{1,0:T(8,128)(2,1)S(1)}, bf16[144,3072]{1,0:T(8,128)(2,1)}, u32[]{:S(2)}) copy-start(bf16[144,3072]{1,0:T(8,128)(2,1)} %get-tuple-element.2) | copy-start | bytes 2654212
  13.2 223.9 %all-gather.3.cloned.1.call-start = ((), (), s32[]{:S(2)}) async-start(), calls=%async_computation | async-start | bytes 4423680 | tf_op jit(solution)/shard_map/all_gather | solution.py:15
  13.8 223.3 %all-gather.5.cloned.1.call-start = ((), (), s32[]{:S(2)}) async-start(), calls=%async_computation.1 | async-start | bytes 7962624 | tf_op jit(solution)/shard_map/all_gather | solution.py:18
Sparse Core Ops, SparseCore 0:
  14.7 218.9 all-reduce.1
Sparse Core Ops, SparseCore 1:
  15.3 34.0 all-gather.2
  51.4 109.7 all-gather.4
where the time goes:
time: 255 us
  waiting for transfers between devices  220 us (86%)
  matrix products  15.6 us (6%)
  between operations  15.5 us (6%)
  other arithmetic  3.27 us (1%)
    psum x1, waiting for transfers between devices, body(): projected = lax.psum(local_terms, ('row', 'col'))  219 us
    dot_general x1, matrix products, body(): lax.dot_general(row_block, lax.all_gather(masked, 'row', axis=0, tiled=Tr...  10.4 us
  transfers between devices with their start and end apart: 3, of which 1 were waited for; matrix products, arithmetic and copies ran while one was open for 1% of the time, Pallas kernels for 0%

commit v1 on v0

--- a/solution.py
+++ b/solution.py
@@ -22,7 +22,8 @@
     local_terms = lax.dot_general(
         masked, vectors, (((0,), (0,)), ((), ())), preferred_element_type=jnp.float32
     )
-    projected = lax.psum(local_terms, ("row", "col"))
+    pieces = lax.all_gather(local_terms, ("row", "col"), axis=0, tiled=False)
+    projected = pieces.sum(axis=0)
     coupled = jnp.dot(
         weighted.astype(jnp.float32),
         projected,

time: 255 us -> 347 us (1.36)
  waiting for transfers between devices: 220 us -> 287 us
  local copies, waits for them, and re-layouts: 0.11 us -> 21.9 us
  other arithmetic: 3.27 us -> 9.22 us
    psum x1 -> x0, waiting for transfers between devices: 219 us -> none  [body(): projected = lax.psum(local_terms, ('row', 'col'))]
    all_gather x0 -> x1, waiting for transfers between devices: none -> 145 us  [body(): pieces = lax.all_gather(local_terms, ('row', 'col'), axis=0, tiled=False)]
    all_gather x1, waiting for transfers between devices: 0.01 us -> 111 us  [body(): lax.all_gather(masked, 'row', axis=0, tiled=True)]
    all_gather x1, waiting for transfers between devices: 0.01 us -> 30.4 us  [body(): row_block = lax.all_gather(weighted, 'col', axis=0, tiled=True)]
    unnamed x8 -> x7, local copies, waits for them, and re-layouts: 0.02 us -> 21.8 us
    reduce_sum x0 -> x1, other arithmetic: none -> 5.7 us  [body(): projected = pieces.sum(axis=0)]
  transfers between devices with their start and end apart: 3 -> 3, of which waited for: 1 -> 3; matrix products, arithmetic and copies ran while one was open for 1% -> 4% of each run, Pallas kernels for 0% -> 0%
where the time goes in v1:
time: 347 us; the launch traced here: 346 us
  waiting for transfers between devices  287 us (83%)
  local copies, waits for them, and re-layouts  21.9 us (6%)
  matrix products  14.4 us (4%)
  between operations  13.8 us (4%)
  other arithmetic  9.22 us (3%)
    all_gather x1, waiting for transfers between devices, body(): pieces = lax.all_gather(local_terms, ('row', 'col'), axis=0, tiled=False)  145 us
    all_gather x1, waiting for transfers between devices, body(): lax.all_gather(masked, 'row', axis=0, tiled=True)  111 us
    all_gather x1, waiting for transfers between devices, body(): row_block = lax.all_gather(weighted, 'col', axis=0, tiled=True)  30.4 us
    unnamed x7, local copies, waits for them, and re-layouts  21.8 us
    dot_general x1, matrix products, body(): lax.dot_general(row_block, lax.all_gather(masked, 'row', axis=0, tiled=Tr...  10.4 us
  transfers between devices with their start and end apart: 3, of which 3 were waited for; matrix products, arithmetic and copies ran while one was open for 4% of the time, Pallas kernels for 0%

profile of v1, /device:TPU:0, one launch (start us, length us, event | category | flops | bytes accessed | tf_op | source)
XLA Modules:
  0.0 346.3 jit_solution(9271300876347314312)
XLA Ops:
  7.2 0.0 copy-start.1
  7.2 0.0 copy-start.2
  7.2 0.0 all-gather.5.cloned.1.call-start
  7.2 0.7 iota_compare_fusion
  8.0 0.1 lt.18
  8.1 2.8 multiply_convert_fusion
  10.8 0.0 all-gather.5.cloned.1.call-update
  10.9 0.0 all-gather.7.cloned.1.call-start
  10.9 0.7 all-gather.7.cloned.1.call-update
  11.6 0.0 all-gather.9.cloned.1.call-start
  11.7 0.0 copy-done.1
  11.7 2.4 fusion.1
  14.0 0.0 all-gather.9.cloned.1.call-update
  14.1 0.0 copy-done.2
  14.1 30.4 %all-gather.5.cloned.1.call-done = bf16[576,3072]{1,0:T(8,128)(2,1)} async-done(((bf16[144,3072]{1,0:T(8,128)(2,1)}), bf16[576,3072]{1,0:T(8,128)(2,1)}) %all-gather.5.cloned.1.call-update) | async-done | bytes 3538960 | tf_op jit(solution)/shard_map/all_gather | solution.py:15
  44.5 111.1 %all-gather.7.cloned.1.call-done = bf16[1152,3072]{1,0:T(8,128)(2,1)} async-done(((bf16[144,3072]{1,0:T(8,128)(2,1)}), bf16[1152,3072]{1,0:T(8,128)(2,1)}) %all-gather.7.cloned.1.call-update) | async-done | bytes 7077904 | tf_op jit(solution)/shard_map/all_gather | solution.py:18
  155.6 10.4 %fusion = f32[576,1152]{1,0:T(8,128)} fusion(bf16[576,3072]{1,0:T(8,128)(2,1)} %all-gather.5.cloned.1.call-done, bf16[1152,3072]{1,0:T(8,128)(2,1)} %all-gather.7.cloned.1.call-done), kind=kOutput, calls=%fused_computation.6 | convolution fusion | flops 4076863488 | bytes 13271040 | tf_op jit(solution)/shard_map/dot_general | solution.py:16
  165.9 144.8 %all-gather.9.cloned.1.call-done = f32[98304,64]{0,1:T(8,128)} async-done(((f32[3072,64]{0,1:T(8,128)}), f32[98304,64]{0,1:T(8,128)}) %all-gather.9.cloned.1.call-update) | async-done | bytes 25165840 | tf_op jit(solution)/shard_map/all_gather | solution.py:25
  310.7 21.8 %copy.7 = f32[8,8,32,3072]{3,2,1,0:T(8,128)S(1)} copy(f32[8,8,32,3072]{3,1,2,0:T(8,128)} %bitcast.11) | data formatting | bytes 50331648
  332.4 0.0 copy-start
  332.5 5.7 %bitcast_reduce_fusion = f32[3072,64]{0,1:T(8,128)S(1)} fusion(f32[8,8,32,3072]{3,2,1,0:T(8,128)S(1)} %copy.7), kind=kLoop, calls=%fused_computation | loop fusion | flops 6094848 | bytes 25952256 | tf_op jit(solution)/shard_map/reduce_sum | solution.py:26
  338.2 0.0 copy-done
  338.2 1.6 convolution_add_fusion
  (1 shorter events, 0.0 us)
Async XLA Ops:
  7.2 4.5 %copy-start.1 = (bf16[144,64]{0,1:T(8,128)(2,1)S(1)}, bf16[144,64]{0,1:T(8,128)(2,1)}, u32[]{:S(2)}) copy-start(bf16[144,64]{0,1:T(8,128)(2,1)} %param.9) | copy-start | bytes 55300
  7.2 6.9 %copy-start.2 = (f32[144]{0:T(256)S(1)}, f32[144]{0:T(256)}, u32[]{:S(2)}) copy-start(f32[144]{0:T(256)} %param.8) | copy-start | bytes 1732
  7.2 37.3 %all-gather.5.cloned.1.call-start = ((), (), s32[]{:S(2)}) async-start(), calls=%async_computation | async-start | bytes 4423680 | tf_op jit(solution)/shard_map/all_gather | solution.py:15
  10.9 144.7 %all-gather.7.cloned.1.call-start = ((), (), s32[]{:S(2)}) async-start(), calls=%async_computation.1 | async-start | bytes 7962624 | tf_op jit(solution)/shard_map/all_gather | solution.py:18
  11.6 299.1 %all-gather.9.cloned.1.call-start = ((), (), s32[]{:S(2)}) async-start(), calls=%async_computation.2 | async-start | bytes 25952256 | tf_op jit(solution)/shard_map/all_gather | solution.py:25
  332.4 5.7 %copy-start = (bf16[144,3072]{1,0:T(8,128)(2,1)S(1)}, bf16[144,3072]{1,0:T(8,128)(2,1)}, u32[]{:S(2)}) copy-start(bf16[144,3072]{1,0:T(8,128)(2,1)} %get-tuple-element.2) | copy-start | bytes 2654212
Sparse Core Ops, SparseCore 0:
  11.0 33.4 all-gather.4
  47.2 108.2 all-gather.6
  158.4 152.2 all-gather.8
